TPU v7x, 32 devices: a whole 2x2x4 slice. The times are simulated.
32 devices in a mesh: seq: 8 (over z, core), head: 4 (over y, x).
Axes of the slice: x: 2, y: 2, z: 4, core: 2. Of those that a mesh axis runs over, the one named last changes fastest.
Arguments:
- grad_output: bfloat16 [8192, 4096], P('seq', 'head'), may hold values from -6 to 6
- out_weight: bfloat16 [4096, 8192], P('seq', 'head'), may hold values from -0.0625 to 0.0625
- ssd_out: bfloat16 [8192, 8192], P('seq', 'head'), may hold values from -520 to 520
- gate: bfloat16 [8192, 8192], P('seq', 'head'), may hold values from -5 to 5
- norm_weight: float32 [8192], P('head'), may hold values from 0.5 to 1.5
- time_step: float32 [128, 8192], P('head', 'seq'), may hold values from 0.01 to 0.1
- log_decay: float32 [128, 8192], P('head', 'seq'), may hold values from -0.7 to 0
- state_in: bfloat16 [8192, 8, 128], P('seq'), may hold values from -1.796875 to 1.796875
- state_out: bfloat16 [8192, 8, 128], P('seq'), may hold values from -1.796875 to 1.796875
- skip: float32 [128], P('head'), may hold values from 0.5 to 1.5
Outputs:
- grad_x: bfloat16 [8192, 8192], P('seq', 'head')
- grad_gate: bfloat16 [8192, 8192], P('seq', 'head')
- grad_out_weight: float32 [4096, 8192], P('seq', 'head')
All inputs are finite; a program needn't handle non-finite values.
Results may differ from a plain program's by a relative error of at most 0.014.
Values may be sent and summed in bfloat16 or wider, within the bound.
A program may use at most 192 MiB of HBM per device.

v0:
```python
import functools
import math

import jax
import jax.numpy as jnp
from jax import lax
from jax.experimental import pallas as pl
from jax.experimental.pallas import tpu as pltpu
from jax.sharding import PartitionSpec as P

HEADS = 128
GROUPS = 8
BLOCK_LEN = 256
MESH = pl.DeviceIdType.MESH
F32 = jnp.float32
BF16 = jnp.bfloat16
ROWS = 16
TILE_ROWS = 64
CHUNK = 128


epsilon = 1e-05


def remote(src, dst, send_sem, recv_sem, **device):
    return pltpu.make_async_remote_copy(
        src_ref=src,
        dst_ref=dst,
        send_sem=send_sem,
        recv_sem=recv_sem,
        device_id=device,
        device_id_type=MESH,
    )


def lane_sum(x):
    total = x[:, 0:128]
    for j in range(1, x.shape[1] // 128):
        total = total + x[:, j * 128 : (j + 1) * 128]
    return total


def mixer_kernel(
    dims,
    g_ref,
    w_ref,
    y_ref,
    z_ref,
    nw_ref,
    ts_ref,
    ld_ref,
    b_ref,
    c_ref,
    skip_ref,
    gate_out,
    gx_out,
    gow_out,
    wfull,
    gfull,
    nbuf,
    acc,
    pair,
    chain,
    pst,
    ownp,
    gt,
    wbuf,
    ybuf,
    zbuf,
    obuf,
    sqp,
    sqx,
    wgx,
    invc,
    cfc,
    cum_row,
    cum_col,
    spread,
    run,
    summ,
    decay,
    rbuf,
    vbuf,
    arrived,
    ag_recv,
    ag_r,
    ag_l,
    ag_p,
    g_recv,
    g_send,
    sq_recv,
    sq_send,
    wg_recv,
    wg_send,
    pair_recv,
    pair_send,
    ch_recv,
    ch_send,
    loc,
    wsem,
    in_sem,
    out_sem,
    swap_recv,
    swap_send,
    st_recv,
    st_send,
    half_recv,
    half_send,
):
    S, H, T, F, Wr, C = dims
    Z = S // 2
    half = Wr // 2
    nsub = F // Wr
    DI = C * H
    TN = min(256, C)
    HL = ld_ref.shape[0]
    HD = C // HL
    GW = min(C, (HEADS // GROUPS) * HD)
    NG = C // GW
    HPG = GW // HD
    NS = b_ref.shape[2]
    CH = C // 2
    chunks = T // CHUNK
    PARTS = 4
    s = lax.axis_index("seq")
    h = lax.axis_index("head")
    z = s // 2
    c = s % 2
    zm = Z - 1 - z
    partner = s + 1 - 2 * c
    others = range(1, H)

    barrier = pltpu.get_barrier_semaphore()
    pl.semaphore_signal(barrier, inc=1, device_id={"seq": partner}, device_id_type=MESH)
    for j in others:
        pl.semaphore_signal(barrier, inc=1, device_id={"head": h ^ j}, device_id_type=MESH)

    @pl.when(z > 0)
    def _():
        pl.semaphore_signal(barrier, inc=1, device_id={"seq": s - 2}, device_id_type=MESH)

    @pl.when(z < Z - 1)
    def _():
        pl.semaphore_signal(barrier, inc=1, device_id={"seq": s + 2}, device_id_type=MESH)

    peers = H + jnp.where(z > 0, 1, 0) + jnp.where(z < Z - 1, 1, 0)
    pl.semaphore_wait(barrier, peers)

    def w_src(k, ch, own):
        return w_ref.at[pl.ds(ch * half, half)] if own else wfull.at[2 * k + c, ch]

    def w_right(k, ch, own=False):
        q = 2 * k + c
        return remote(
            w_src(k, ch, own), wfull.at[q, ch], ag_r.at[k, ch], ag_recv.at[q, ch], seq=s + 2
        )

    def w_left(k, ch, own=False):
        q = 2 * k + c
        return remote(
            w_src(k, ch, own), wfull.at[q, ch], ag_l.at[k, ch], ag_recv.at[q, ch], seq=s - 2
        )

    def w_swap(k, ch, own=False):
        q = 2 * k + c
        return remote(
            w_src(k, ch, own), wfull.at[q, ch], ag_p.at[k, ch], ag_recv.at[q, ch], seq=partner
        )

    def w_arrived(q, ch):
        remote(
            wfull.at[q, ch], wfull.at[q, ch], ag_p.at[0, 0], ag_recv.at[q, ch], seq=partner
        ).wait_recv()

    for ch in range(2):

        @pl.when(z < Z - 1)
        def _():
            w_right(z, ch, True).start()

        @pl.when(z > 0)
        def _():
            w_left(z, ch, True).start()

        w_swap(z, ch, True).start()

    def g_own(sub, hf):
        return g_ref.at[:, pl.ds(sub * Wr + hf * half, half)]

    def g_local(sub, hf):
        return pltpu.make_async_copy(
            g_own(sub, hf), gfull.at[h * nsub + sub, hf], loc.at[sub, hf]
        )

    for sub in range(nsub):
        for hf in range(2):
            g_local(sub, hf).start()

    tiles = T // TILE_ROWS

    def fetch(t, slot):
        rows = pl.ds(t * TILE_ROWS, TILE_ROWS)
        return (
            pltpu.make_async_copy(y_ref.at[rows], ybuf.at[slot], in_sem.at[0, slot]),
            pltpu.make_async_copy(z_ref.at[rows], zbuf.at[slot], in_sem.at[1, slot]),
        )

    def stream(body):
        for copy in fetch(0, 0):
            copy.start()

        @pl.loop(0, tiles)
        def _(t):
            slot = t % 2

            @pl.when(t + 1 < tiles)
            def _():
                for copy in fetch(t + 1, 1 - slot):
                    copy.start()

            for copy in fetch(t, slot):
                copy.wait()
            body(t, slot)

    def square_tile(t, slot):
        @pl.loop(0, TILE_ROWS // ROWS)
        def _(r):
            rows = pl.ds(r * ROWS, ROWS)
            at = pl.ds(t * TILE_ROWS + r * ROWS, ROWS)
            gv = zbuf[slot, rows, :].astype(F32)
            gated = ybuf[slot, rows, :].astype(F32) * (gv * jax.nn.sigmoid(gv))
            acc[at, :] = gated
            sqp[at, :] = lane_sum(gated * gated)

    stream(square_tile)

    def share(buf, send, recv):
        buf[h] = jnp.broadcast_to(jnp.sum(sqp[...].T, axis=0, keepdims=True), (8, T))
        for j in others:
            remote(buf.at[h], buf.at[h], send.at[j], recv.at[h], head=h ^ j).start()

    def shared(buf, send, recv):
        for j in others:
            remote(buf.at[h ^ j], buf.at[h ^ j], send.at[j], recv.at[h ^ j], head=h ^ j).wait_recv()
        total = buf[0, 0:1, :]
        for j in others:
            total = total + buf[j, 0:1, :]
        for j in others:
            remote(buf.at[h], buf.at[h], send.at[j], recv.at[h], head=h ^ j).wait_send()
        return total

    share(sqx, sq_send, sq_recv)

    def g_to(j, sub, hf):
        q = h * nsub + sub
        return remote(
            g_own(sub, hf), gfull.at[q, hf], g_send.at[j, sub, hf], g_recv.at[q, hf], head=h ^ j
        )

    def g_relay(j, frm, sub, hf):
        q = (h ^ frm) * nsub + sub
        return remote(
            gfull.at[q, hf], gfull.at[q, hf], g_send.at[3, sub, hf], g_recv.at[q, hf], head=h ^ j
        )

    def g_arrived(j, sub, hf):
        q = (h ^ j) * nsub + sub
        remote(
            gfull.at[q, hf], gfull.at[q, hf], g_send.at[j, sub, hf], g_recv.at[q, hf], head=h ^ j
        ).wait_recv()

    subs = range(nsub)
    if H == 4:
        for sub in subs:
            g_to(1, sub, 0).start()
            g_to(2, sub, 1).start()
    else:
        for j in others:
            for sub in subs:
                for hf in range(2):
                    g_to(j, sub, hf).start()

    inv_row = lax.rsqrt(shared(sqx, sq_send, sq_recv) / DI + epsilon)
    invc[...] = jnp.broadcast_to(inv_row, (128, T)).T

    @pl.loop(0, T // ROWS)
    def _(r):
        at = pl.ds(r * ROWS, ROWS)
        nbuf[at, :] = (acc[at, :] * invc[at, 0:1] * nw_ref[...]).astype(BF16)

    for sub in subs:
        for hf in range(2):
            g_local(sub, hf).wait()
    if H == 4:
        for sub in subs:
            g_arrived(1, sub, 0)
            g_relay(2, 1, sub, 0).start()
        for sub in subs:
            g_arrived(2, sub, 1)
            g_relay(1, 2, sub, 1).start()
        for sub in subs:
            g_to(1, sub, 1).start()
            g_to(2, sub, 0).start()


    tri = (
        lax.broadcasted_iota(jnp.int32, (CHUNK, CHUNK), 0)
        <= lax.broadcasted_iota(jnp.int32, (CHUNK, CHUNK), 1)
    ).astype(F32)
    cum_row[...] = jnp.zeros_like(cum_row)
    for q in range(chunks):
        cols = slice(q * CHUNK, (q + 1) * CHUNK)
        cum_row[0:HL, cols] = jnp.dot(
            ld_ref[:, cols], tri, precision=lax.Precision.HIGHEST, preferred_element_type=F32
        )
    cum_col[...] = cum_row[...].T
    spread[...] = (
        lax.broadcasted_iota(jnp.int32, (128, C), 0)
        == lax.broadcasted_iota(jnp.int32, (128, C), 1) // HD
    ).astype(BF16)

    def widen(x, g):
        high = x.astype(BF16)
        low = (x - high.astype(F32)).astype(BF16)
        onto = spread[:, g * GW : (g + 1) * GW]
        return jnp.dot(high, onto, preferred_element_type=F32) + jnp.dot(
            low, onto, preferred_element_type=F32
        )

    def last_of(q):
        return cum_col[pl.ds(q * CHUNK + CHUNK - 1, 1), :]

    def pair_copy(k, cx, d, ch):
        return remote(
            pst.at[d, ch], pair.at[k, cx], pair_send.at[d, ch], pair_recv.at[k, cx], seq=partner
        )

    def rs_prep(k, cx, d, ch, slot):
        gt[0:half, :] = gfull[2 * k + 1 - c, cx].T
        gt[half:Wr, :] = gfull[2 * k + c, cx].T

        @pl.loop(0, C // TN)
        def _(t):
            cols = pl.ds(pl.multiple_of(t * TN, TN), TN)
            part = jnp.dot(gt[...], nbuf[:, cols], preferred_element_type=F32)
            pst[d, ch, :, cols] = part[:half].astype(BF16)
            ownp[slot, :, cols] = part[half:]

        pair_copy(k, cx, d, ch).start()

    def chain_right(k, cx):
        return remote(
            chain.at[k, cx], chain.at[k, cx], ch_send.at[k, cx], ch_recv.at[k, cx], seq=s + 2
        )

    def chain_left(k, cx):
        to = jnp.where(k == z - 1, Z, k)
        return remote(
            chain.at[k, cx], chain.at[to, cx], ch_send.at[k, cx], ch_recv.at[to, cx], seq=s - 2
        )

    def chain_arrived(k, cx):
        remote(
            chain.at[k, cx], chain.at[k, cx], ch_send.at[0, 0], ch_recv.at[k, cx], seq=partner
        ).wait_recv()

    def rs_sum(k, cx, d, ch, chained):
        pair_copy(k, cx, d, ch).wait_recv()

        @pl.when(chained)
        def _():
            chain_arrived(k, cx)

            @pl.loop(0, half // ROWS)
            def _(r):
                at = pl.ds(r * ROWS, ROWS)
                chain[k, cx, at, :] = (
                    ownp[d, at, :] + pair[k, cx, at, :].astype(F32) + chain[k, cx, at, :].astype(F32)
                ).astype(BF16)

        @pl.when(jnp.logical_not(chained))
        def _():
            @pl.loop(0, half // ROWS)
            def _(r):
                at = pl.ds(r * ROWS, ROWS)
                chain[k, cx, at, :] = (ownp[d, at, :] + pair[k, cx, at, :].astype(F32)).astype(BF16)

    def half_of(k, ch):
        if H != 4:
            return ch
        return jnp.where((2 * k * Wr // F) ^ h == 2, 1 - ch, ch)

    near = jnp.minimum(z, zm)

    def plane_of(p):
        d = (p + 1) // 2
        close = jnp.where(p % 2 == 1, z - d, z + d)
        far = jnp.where(z < zm, z + (p - near), z - (p - near))
        return jnp.where(p <= 2 * near, close, far)

    def w_load(src, par, ch):
        return pltpu.make_async_copy(src, wbuf.at[par, ch], wsem.at[par, ch])

    def project(p, first):
        k = plane_of(p)
        for ch in range(2):
            w_arrived(2 * k + 1 - c, ch)
        for par in range(2):
            for ch in range(2):
                mine = jnp.logical_and(k == z, c == par)

                @pl.when(mine)
                def _():
                    w_load(w_ref.at[pl.ds(ch * half, half)], par, ch).start()

                @pl.when(jnp.logical_not(mine))
                def _():
                    w_load(wfull.at[2 * k + par, ch], par, ch).start()

        for par in range(2):
            for ch in range(2):
                w_load(wfull.at[2 * k + par, ch], par, ch).wait()

        @pl.loop(0, C // TN)
        def _(t):
            cols = pl.ds(pl.multiple_of(t * TN, TN), TN)
            total = None if first else acc[:, cols]
            for par in range(2):
                for ch in range(2):
                    part = jnp.dot(
                        gfull[2 * k + par, ch], wbuf[par, ch, :, cols], preferred_element_type=F32
                    )
                    total = part if total is None else total + part
            acc[:, cols] = total

    @pl.loop(2, 2 * Z)
    def _(i):
        slot = i // 2
        ch = i % 2

        @pl.when(z - slot >= 0)
        def _():
            k = z - slot
            w_arrived(2 * k + c, ch)

            @pl.when(z < Z - 1)
            def _():
                w_right(k, ch).start()

            w_swap(k, ch).start()

        @pl.when(z + slot <= Z - 1)
        def _():
            k = z + slot
            w_arrived(2 * k + c, ch)

            @pl.when(z > 0)
            def _():
                w_left(k, ch).start()

            w_swap(k, ch).start()

        @pl.when(i == 2)
        def _():
            for j in (others if H != 4 else (3,)):
                for sub in subs:
                    for hf in range(2):
                        g_arrived(j, sub, hf)

        if H == 4:

            @pl.when(i == 3)
            def _():
                for sub in subs:
                    g_arrived(1, sub, 1)
                    g_arrived(2, sub, 0)

        go_right = jnp.logical_and(slot > z, z < Z - 1)
        go_left = jnp.logical_and(slot > zm, z > 0)
        kr = Z + z - slot
        kl = slot - Z + z

        @pl.when(go_right)
        def _():
            @pl.when(slot - 1 > z)
            def _():
                pair_copy(kr, 0, 0, ch).wait_send()

            rs_prep(kr, half_of(kr, ch), 0, ch, 0)

        @pl.when(go_left)
        def _():
            @pl.when(slot - 1 > zm)
            def _():
                pair_copy(kl, 0, 1, ch).wait_send()

            rs_prep(kl, half_of(kl, ch), 1, ch, 1)

        @pl.when(go_right)
        def _():
            cx = half_of(kr, ch)
            rs_sum(kr, cx, 0, ch, z > 0)
            chain_right(kr, cx).start()

        @pl.when(go_left)
        def _():
            cx = half_of(kl, ch)
            rs_sum(kl, cx, 1, ch, z < Z - 1)
            chain_left(kl, cx).start()

        @pl.when(i == 4)
        def _():
            project(0, True)

        lo = jnp.where(i == 4, 1, jnp.where(i == 5, 2, slot))
        hi = jnp.where(
            i == 4, 2, jnp.where(i == 5, 3, jnp.where((slot >= 3) & (ch == 1), slot + 1, slot))
        )
        hi = jnp.where(i < 4, lo, jnp.minimum(hi, Z - 1))

        @pl.loop(lo, hi)
        def _(p):
            project(p, False)

    project(Z - 1, False)

    @pl.loop(0, T // ROWS)
    def _(r):
        at = pl.ds(r * ROWS, ROWS)
        sqp[at, :] = lane_sum(acc[at, :] * nbuf[at, :].astype(F32))

    share(wgx, wg_send, wg_recv)
    for ch in range(2):

        @pl.when(Z - 1 > z)
        def _():
            pair_copy(z, ch, 0, ch).wait_send()

        rs_prep(z, ch, 0, ch, ch)

    weighted = shared(wgx, wg_send, wg_recv) / DI
    cfc[...] = jnp.broadcast_to(weighted, (128, T)).T * invc[...] * invc[...]

    def put(t, slot):
        rows = pl.ds(t * TILE_ROWS, TILE_ROWS)
        return pltpu.make_async_copy(obuf.at[slot], gate_out.at[rows], out_sem.at[0, slot])

    def grad_tile(t, slot):
        @pl.when(t >= 2)
        def _():
            put(t - 2, slot).wait()

        @pl.loop(0, TILE_ROWS // ROWS)
        def _(r):
            rows = pl.ds(r * ROWS, ROWS)
            at = pl.ds(t * TILE_ROWS + r * ROWS, ROWS)
            gv = zbuf[slot, rows, :].astype(F32)
            values = ybuf[slot, rows, :].astype(F32)
            sig = jax.nn.sigmoid(gv)
            silu = gv * sig
            gg = invc[at, 0:1] * nw_ref[...] * acc[at, :] - values * silu * cfc[at, 0:1]
            obuf[slot, rows, :] = (gg * values * sig * (1.0 + gv * (1.0 - sig))).astype(BF16)
            nbuf[at, :] = (gg * silu).astype(BF16)

        put(t, slot).start()

    stream(grad_tile)
    for t in (tiles - 2, tiles - 1):
        put(t, t % 2).wait()

    pads = jnp.zeros((128 - HL, T), F32)
    cfc[...] = jnp.concatenate([ts_ref[...], pads], axis=0).T
    per = 2 * half // CHUNK

    def inside(q):
        plane = lax.rem(z + 1 + q // per, Z)
        r = q % per
        rows = half // CHUNK
        return plane, r // rows, pl.ds(pl.multiple_of((r % rows) * CHUNK, CHUNK), CHUNK)

    run[...] = jnp.zeros_like(run)

    @pl.loop(0, chunks, init_carry=jnp.zeros((1, 128), F32))
    def tail(step, later):
        q = chunks - 1 - step
        at = pl.ds(pl.multiple_of(q * CHUNK, CHUNK), CHUNK)
        total = last_of(q)
        sqp[at, :] = total - cum_col[at, :] + later
        grow = jnp.exp(cum_col[at, :])
        keep = jnp.exp(jnp.broadcast_to(total, (8, 128)))
        plane, hf, rows = inside(q)
        for g in range(NG):
            cols = slice(g * GW, (g + 1) * GW)
            scaled = (widen(grow, g) * nbuf[at, cols].astype(F32)).astype(BF16)
            state = jnp.dot(c_ref[g, at, :].T, scaled, preferred_element_type=F32)
            pair[plane, hf, rows, cols] = run[:, cols].astype(BF16)
            run[:, cols] = state + widen(keep, g)[0:1, :] * run[:, cols]
        return later + total

    summ[c] = run[...].astype(BF16)
    keep_all = jnp.exp(jnp.broadcast_to(tail, (8, 128)))
    for g in range(NG):
        decay[c, :, g * GW : (g + 1) * GW] = widen(keep_all, g)

    def swaps():
        return (
            remote(summ.at[c], summ.at[c], swap_send.at[0], swap_recv.at[0], seq=partner),
            remote(decay.at[c], decay.at[c], swap_send.at[1], swap_recv.at[1], seq=partner),
        )

    for copy in swaps():
        copy.start()

    def state_left(part):
        rows = pl.ds(part * (NS // PARTS), NS // PARTS)
        return remote(
            vbuf.at[rows], rbuf.at[c, rows], st_send.at[part], st_recv.at[part], seq=s - 2
        )

    def state_swap(part):
        rows = pl.ds(part * (NS // PARTS), NS // PARTS)
        return remote(
            rbuf.at[c, rows], rbuf.at[c, rows], half_send.at[part], half_recv.at[part], seq=partner
        )

    mine_cols = pl.ds(pl.multiple_of(c * CH, CH), CH)

    def state_step(part):
        rows = pl.ds(part * (NS // PARTS), NS // PARTS)

        @pl.when(z < Z - 1)
        def _():
            state_left(part).wait_recv()
            state_swap(part).start()

        @pl.when(z > 0)
        def _():
            first_keep = decay[0, 0:1, mine_cols]
            here = summ[0, rows, mine_cols].astype(F32) + first_keep * summ[
                1, rows, mine_cols
            ].astype(F32)

            @pl.when(z < Z - 1)
            def _():
                vbuf[rows, :] = (
                    here
                    + first_keep * decay[1, 0:1, mine_cols] * rbuf[c, rows, :].astype(F32)
                ).astype(BF16)

            @pl.when(z == Z - 1)
            def _():
                vbuf[rows, :] = here.astype(BF16)

            state_left(part).start()

    upper = lax.broadcasted_iota(jnp.int32, (CHUNK, CHUNK), 1) >= lax.broadcasted_iota(
        jnp.int32, (CHUNK, CHUNK), 0
    )
    lane = lax.broadcasted_iota(jnp.int32, (CHUNK, 2 * HD), 1)

    @pl.loop(0, chunks)
    def _(q):
        @pl.when(q == 0)
        def _():
            for copy in swaps():
                copy.wait_recv()

        for part in range(PARTS):

            @pl.when(q == jnp.minimum(zm + part, chunks - 1))
            def _():
                state_step(part)

        at = pl.ds(pl.multiple_of(q * CHUNK, CHUNK), CHUNK)
        plane, hf, rows = inside(q)
        cum = cum_col[at, :]
        fade = jnp.exp(last_of(q) - cum)
        steps = cfc[at, :]
        skips = jnp.broadcast_to(skip_ref[...], (8, 128))
        for g in range(NG):
            b = b_ref[g, at, :]
            scores = lax.dot_general(
                b, c_ref[g, at, :], (((1,), (1,)), ((), ())), preferred_element_type=F32
            )
            scores = jnp.where(upper, scores, 0.0)
            cols = slice(g * GW, (g + 1) * GW)
            acc[at, cols] = widen(fade, g) * jnp.dot(
                b, pair[plane, hf, rows, cols], preferred_element_type=F32
            )
            for j in range(HPG // 2):
                weights = []
                for head in (g * HPG + 2 * j, g * HPG + 2 * j + 1):
                    gap = cum_row[head : head + 1, at] - cum[:, head : head + 1]
                    weights.append((scores * jnp.exp(jnp.minimum(gap, 0.0))).astype(BF16))
                span = slice(g * GW + 2 * j * HD, g * GW + 2 * (j + 1) * HD)
                both = nbuf[at, span]
                zero = jnp.zeros_like(both)
                stacked = jnp.concatenate(
                    [jnp.where(lane < HD, both, zero), jnp.where(lane < HD, zero, both)], axis=0
                )
                acc[at, span] = acc[at, span] + jnp.dot(
                    jnp.concatenate(weights, axis=1), stacked, preferred_element_type=F32
                )
            acc[at, cols] = widen(steps, g) * acc[at, cols] + widen(skips, g)[0:1, :] * nbuf[
                at, cols
            ].astype(F32)

    @pl.when(z < Z - 1)
    def _():
        for part in range(PARTS):
            rows = pl.ds(part * (NS // PARTS), NS // PARTS)
            remote(
                rbuf.at[1 - c, rows],
                rbuf.at[1 - c, rows],
                half_send.at[part],
                half_recv.at[part],
                seq=partner,
            ).wait_recv()

    @pl.when(z == Z - 1)
    def _():
        rbuf[...] = jnp.zeros_like(rbuf)

    for side in range(2):
        cols = slice(side * CH, (side + 1) * CH)
        later = rbuf[side].astype(F32)

        @pl.when(c == 1)
        def _():
            arrived[:, cols] = later.astype(BF16)

        @pl.when(c == 0)
        def _():
            arrived[:, cols] = (
                summ[1, :, cols].astype(F32) + decay[1, 0:1, cols] * later
            ).astype(BF16)

    def put_x(t, slot):
        rows = pl.ds(t * TILE_ROWS, TILE_ROWS)
        return pltpu.make_async_copy(ybuf.at[slot], gx_out.at[rows], out_sem.at[1, slot])

    @pl.loop(0, tiles)
    def _(t):
        slot = t % 2
        at = pl.ds(pl.multiple_of(t * TILE_ROWS, TILE_ROWS), TILE_ROWS)

        @pl.when(t >= 2)
        def _():
            put_x(t - 2, slot).wait()

        factor = cfc[at, :] * jnp.exp(sqp[at, :])
        for g in range(NG):
            cols = slice(g * GW, (g + 1) * GW)
            ybuf[slot, :, cols] = (
                acc[at, cols]
                + widen(factor, g)
                * jnp.dot(b_ref[g, at, :], arrived[:, cols], preferred_element_type=F32)
            ).astype(BF16)
        put_x(t, slot).start()

    scale = 1.0 / math.sqrt(T * S)

    def gow_copy(ch):
        rows = pl.ds(ch * half, half)
        return pltpu.make_async_copy(ownp.at[ch], gow_out.at[rows], out_sem.at[0, ch])

    for ch in range(2):
        pair_copy(z, ch, 0, ch).wait_recv()

        @pl.loop(0, half // ROWS)
        def _(r):
            at = pl.ds(r * ROWS, ROWS)
            ownp[ch, at, :] = ownp[ch, at, :] + pair[z, ch, at, :].astype(F32)

    for first, from_slot in ((0, z), (Z - 1, Z)):
        for step in range(2):

            @pl.when(z != first)
            def _():
                ch = half_of(z, step)
                chain_arrived(from_slot, ch)

                @pl.loop(0, half // ROWS)
                def _(r):
                    at = pl.ds(r * ROWS, ROWS)
                    ownp[ch, at, :] = ownp[ch, at, :] + chain[from_slot, ch, at, :].astype(F32)

    for ch in range(2):

        @pl.loop(0, half // ROWS)
        def _(r):
            at = pl.ds(r * ROWS, ROWS)
            ownp[ch, at, :] = ownp[ch, at, :] * scale

        gow_copy(ch).start()

    for t in (tiles - 2, tiles - 1):
        put_x(t, t % 2).wait()

    for copy in swaps():
        copy.wait_send()
    for part in range(PARTS):

        @pl.when(z < Z - 1)
        def _():
            state_swap(part).wait_send()

        @pl.when(z > 0)
        def _():
            state_left(part).wait_send()

    for ch in range(2):
        pair_copy(z, ch, 0, ch).wait_send()

        @pl.when(z > 0)
        def _():
            pair_copy(z, ch, 1, ch).wait_send()

        @pl.loop(0, Z)
        def _(k):
            w_swap(k, ch).wait_send()

            @pl.when(jnp.logical_and(k <= z, z < Z - 1))
            def _():
                w_right(k, ch).wait_send()

            @pl.when(jnp.logical_and(k >= z, z > 0))
            def _():
                w_left(k, ch).wait_send()

            @pl.when(k > z)
            def _():
                chain_right(k, ch).wait_send()

            @pl.when(k < z)
            def _():
                chain_left(k, ch).wait_send()

    for sub in subs:
        if H == 4:
            g_relay(2, 1, sub, 0).wait_send()
            g_relay(1, 2, sub, 1).wait_send()
        for j in others if H != 4 else (1, 2):
            for hf in range(2):
                g_to(j, sub, hf).wait_send()
    for ch in range(2):
        gow_copy(ch).wait()


def mixer(
    grad_output,
    out_weight,
    ssd_out,
    gate,
    norm_weight,
    time_step,
    log_decay,
    state_in,
    state_out,
    skip,
):
    S, H = lax.axis_size("seq"), lax.axis_size("head")
    T, F = grad_output.shape
    Wr, C = out_weight.shape
    Z = S // 2
    half = Wr // 2
    nsub = F // Wr
    heads_here = time_step.shape[0]
    groups_here = max(1, heads_here * GROUPS // HEADS)
    first_group = lax.axis_index("head") * heads_here // (HEADS // GROUPS)

    def picked(x):
        return lax.dynamic_slice_in_dim(x, first_group, groups_here, 1).transpose(1, 0, 2)

    skip_row = jnp.pad(skip, (0, 128 - heads_here)).reshape(1, 128)
    NS = state_in.shape[2]
    hbm = pl.BlockSpec(memory_space=pl.ANY)
    vmem = pl.BlockSpec(memory_space=pltpu.VMEM)
    dma = pltpu.SemaphoreType.DMA
    flops = 4 * T * F * H * C
    outs = pl.pallas_call(
        functools.partial(mixer_kernel, (S, H, T, F, Wr, C)),
        out_shape=(
            jax.ShapeDtypeStruct((T, C), BF16),
            jax.ShapeDtypeStruct((T, C), BF16),
            jax.ShapeDtypeStruct((Wr, C), F32),
            jax.ShapeDtypeStruct((S, 2, half, C), BF16),
        ),
        in_specs=[hbm] * 4 + [vmem] * 6,
        out_specs=(hbm,) * 4,
        scratch_shapes=[
            pltpu.VMEM((S, 2, T, half), BF16),
            pltpu.VMEM((T, C), BF16),
            pltpu.VMEM((T, C), F32),
            pltpu.VMEM((Z, 2, half, C), BF16),
            pltpu.VMEM((Z + 1, 2, half, C), BF16),
            pltpu.VMEM((2, 2, half, C), BF16),
            pltpu.VMEM((2, half, C), F32),
            pltpu.VMEM((Wr, T), BF16),
            pltpu.VMEM((2, 2, half, C), BF16),
            pltpu.VMEM((2, TILE_ROWS, C), BF16),
            pltpu.VMEM((2, TILE_ROWS, C), BF16),
            pltpu.VMEM((2, TILE_ROWS, C), BF16),
            pltpu.VMEM((T, 128), F32),
            pltpu.VMEM((H, 8, T), F32),
            pltpu.VMEM((H, 8, T), F32),
            pltpu.VMEM((T, 128), F32),
            pltpu.VMEM((T, 128), F32),
            pltpu.VMEM((128, T), F32),
            pltpu.VMEM((T, 128), F32),
            pltpu.VMEM((128, C), BF16),
            pltpu.VMEM((NS, C), F32),
            pltpu.VMEM((2, NS, C), BF16),
            pltpu.VMEM((2, 8, C), F32),
            pltpu.VMEM((2, NS, C // 2), BF16),
            pltpu.VMEM((NS, C // 2), BF16),
            pltpu.VMEM((NS, C), BF16),
            dma((S, 2)),
            dma((Z, 2)),
            dma((Z, 2)),
            dma((Z, 2)),
            dma((S, 2)),
            dma((H, nsub, 2)),
            dma((H,)),
            dma((H,)),
            dma((H,)),
            dma((H,)),
            dma((Z, 2)),
            dma((2, 2)),
            dma((Z + 1, 2)),
            dma((Z, 2)),
            dma((nsub, 2)),
            dma((2, 2)),
            dma((2, 2)),
            dma((2, 2)),
            dma((2,)),
            dma((2,)),
            dma((4,)),
            dma((4,)),
            dma((4,)),
            dma((4,)),
        ],
        compiler_params=pltpu.CompilerParams(
            collective_id=0, has_side_effects=True, vmem_limit_bytes=67043328
        ),
        cost_estimate=pl.CostEstimate(flops=flops, bytes_accessed=64 << 20, transcendentals=0),
        name="mixer",
    )(
        grad_output,
        out_weight,
        ssd_out,
        gate,
        norm_weight.reshape(1, C),
        time_step,
        log_decay,
        picked(state_in),
        picked(state_out),
        skip_row,
    )
    grad_gate, grad_x, grad_out_weight, _ = outs
    return grad_x, grad_gate, grad_out_weight


def solution(mesh):
    return jax.shard_map(
        mixer,
        mesh=mesh,
        in_specs=(
            P("seq", "head"),
            P("seq", "head"),
            P("seq", "head"),
            P("seq", "head"),
            P("head"),
            P("head", "seq"),
            P("head", "seq"),
            P("seq", None, None),
            P("seq", None, None),
            P("head"),
        ),
        out_specs=(P("seq", "head"), P("seq", "head"), P("seq", "head")),
        check_vma=False,
    )
```

profile of v0, /device:TPU:0, one launch (start us, length us, event | category | flops | bytes accessed | tf_op | source)
XLA Modules:
  0.0 256.6 jit_solution(3315468038265472801)
XLA Ops:
  0.6 1.2 pad_bitcast_fusion.skip_ref
  1.8 3.3 %constant_dynamic-slice_fusion = (bf16[1024,2,128]{2,1,0:T(2,128)(2,1)S(1)}, bf16[1024,2,128]{2,1,0:T(2,128)(2,1)S(1)}) fusion(bf16[1024,8,128]{2,1,0:T(8,128)(2,1)} %param.18, s32[]{:T(128)S(6)} %select_n.10, bf16[1024,8,128]{2,1,0:T(8,128)(2,1)} %param.17), kind=kLoop, calls=%fused_computation.3 | loop fusion | bytes 2097156 | tf_op jit(solution)/shard_map/dynamic_slice | solution.py:873
  5.1 0.9 copy.19
  6.0 0.9 copy.20
  6.8 239.1 %mixer.1 = (bf16[1024,2048]{1,0:T(8,128)(2,1)}, bf16[1024,2048]{1,0:T(8,128)(2,1)}, f32[512,2048]{1,0:T(8,128)}, bf16[8,2,256,2048]{3,2,1,0:T(8,128)(2,1)}) custom-call(bf16[1024,1024]{1,0:T(8,128)(2,1)} %g_ref.1, bf16[512,2048]{1,0:T(8,128)(2,1)} %w_ref.1, bf16[1024,2048]{1,0:T(8,128)(2,1)} %y_ref.1, bf16[1024,2048]{1,0:T(8,128)(2,1)} %z_ref.1, ...), custom_call_target="tpu_custom_call" | custom-call | flops 34359738368 | bytes 67108864 | tf_op jit(solution)/shard_map/mixer/pallas_call | solution.py:881
  245.9 0.0 copy-start.1
  245.9 4.9 %copy.24 = bf16[1024,2048]{1,0:T(8,128)(2,1)} copy(bf16[1024,2048]{1,0:T(8,128)(2,1)} %get-tuple-element.14) | data formatting | bytes 8388608
  250.9 0.0 copy-done.1
  250.9 0.0 copy-start
  250.9 2.1 copy.25
  253.0 1.6 copy-done
  254.6 2.0 copy.26
Async XLA Ops:
  245.9 5.0 %copy-start.1 = (bf16[1024,2048]{1,0:T(8,128)(2,1)S(1)}, bf16[1024,2048]{1,0:T(8,128)(2,1)}, u32[]{:S(2)}) copy-start(bf16[1024,2048]{1,0:T(8,128)(2,1)} %get-tuple-element.15) | copy-start | bytes 12582916
  250.9 3.7 %copy-start = (f32[512,2048]{1,0:T(8,128)S(1)}, f32[512,2048]{1,0:T(8,128)}, u32[]{:S(2)}) copy-start(f32[512,2048]{1,0:T(8,128)} %get-tuple-element.16) | copy-start | bytes 12582916
where the time goes:
time: 257 us
  Pallas kernels  239 us (93%)
  local copies, waits for them, and re-layouts  16.9 us (7%)
    pallas_call x1, Pallas kernels, mixer(): pl.pallas_call(functools.partial(mixer_kernel, (S, H, T, F, Wr, C)), out_...  239 us
    unnamed x9, local copies, waits for them, and re-layouts  12.4 us

commit v1 on v0

--- a/solution.py
+++ b/solution.py
@@ -49,8 +49,8 @@
     nw_ref,
     ts_ref,
     ld_ref,
-    b_ref,
-    c_ref,
+    si_ref,
+    so_ref,
     skip_ref,
     gate_out,
     gx_out,
@@ -82,6 +82,9 @@
     rbuf,
     vbuf,
     arrived,
+    raw,
+    b_ref,
+    c_ref,
     ag_recv,
     ag_r,
     ag_l,
@@ -106,6 +109,7 @@
     st_send,
     half_recv,
     half_send,
+    late_sem,
 ):
     S, H, T, F, Wr, C = dims
     Z = S // 2
@@ -118,7 +122,7 @@
     GW = min(C, (HEADS // GROUPS) * HD)
     NG = C // GW
     HPG = GW // HD
-    NS = b_ref.shape[2]
+    NS = si_ref.shape[2]
     CH = C // 2
     chunks = T // CHUNK
     PARTS = 4
@@ -127,6 +131,7 @@
     z = s // 2
     c = s % 2
     zm = Z - 1 - z
+    first_group = h * HL // (HEADS // GROUPS)
     partner = s + 1 - 2 * c
     others = range(1, H)
 
@@ -195,61 +200,6 @@
     for sub in range(nsub):
         for hf in range(2):
             g_local(sub, hf).start()
-
-    tiles = T // TILE_ROWS
-
-    def fetch(t, slot):
-        rows = pl.ds(t * TILE_ROWS, TILE_ROWS)
-        return (
-            pltpu.make_async_copy(y_ref.at[rows], ybuf.at[slot], in_sem.at[0, slot]),
-            pltpu.make_async_copy(z_ref.at[rows], zbuf.at[slot], in_sem.at[1, slot]),
-        )
-
-    def stream(body):
-        for copy in fetch(0, 0):
-            copy.start()
-
-        @pl.loop(0, tiles)
-        def _(t):
-            slot = t % 2
-
-            @pl.when(t + 1 < tiles)
-            def _():
-                for copy in fetch(t + 1, 1 - slot):
-                    copy.start()
-
-            for copy in fetch(t, slot):
-                copy.wait()
-            body(t, slot)
-
-    def square_tile(t, slot):
-        @pl.loop(0, TILE_ROWS // ROWS)
-        def _(r):
-            rows = pl.ds(r * ROWS, ROWS)
-            at = pl.ds(t * TILE_ROWS + r * ROWS, ROWS)
-            gv = zbuf[slot, rows, :].astype(F32)
-            gated = ybuf[slot, rows, :].astype(F32) * (gv * jax.nn.sigmoid(gv))
-            acc[at, :] = gated
-            sqp[at, :] = lane_sum(gated * gated)
-
-    stream(square_tile)
-
-    def share(buf, send, recv):
-        buf[h] = jnp.broadcast_to(jnp.sum(sqp[...].T, axis=0, keepdims=True), (8, T))
-        for j in others:
-            remote(buf.at[h], buf.at[h], send.at[j], recv.at[h], head=h ^ j).start()
-
-    def shared(buf, send, recv):
-        for j in others:
-            remote(buf.at[h ^ j], buf.at[h ^ j], send.at[j], recv.at[h ^ j], head=h ^ j).wait_recv()
-        total = buf[0, 0:1, :]
-        for j in others:
-            total = total + buf[j, 0:1, :]
-        for j in others:
-            remote(buf.at[h], buf.at[h], send.at[j], recv.at[h], head=h ^ j).wait_send()
-        return total
-
-    share(sqx, sq_send, sq_recv)
 
     def g_to(j, sub, hf):
         q = h * nsub + sub
@@ -280,17 +230,61 @@
                 for hf in range(2):
                     g_to(j, sub, hf).start()
 
-    inv_row = lax.rsqrt(shared(sqx, sq_send, sq_recv) / DI + epsilon)
-    invc[...] = jnp.broadcast_to(inv_row, (128, T)).T
-
-    @pl.loop(0, T // ROWS)
-    def _(r):
-        at = pl.ds(r * ROWS, ROWS)
-        nbuf[at, :] = (acc[at, :] * invc[at, 0:1] * nw_ref[...]).astype(BF16)
-
-    for sub in subs:
-        for hf in range(2):
-            g_local(sub, hf).wait()
+    tiles = T // TILE_ROWS
+
+    def fetch(t, slot):
+        rows = pl.ds(t * TILE_ROWS, TILE_ROWS)
+        return (
+            pltpu.make_async_copy(y_ref.at[rows], ybuf.at[slot], in_sem.at[0, slot]),
+            pltpu.make_async_copy(z_ref.at[rows], zbuf.at[slot], in_sem.at[1, slot]),
+        )
+
+    def stream(body):
+        for copy in fetch(0, 0):
+            copy.start()
+
+        @pl.loop(0, tiles)
+        def _(t):
+            slot = t % 2
+
+            @pl.when(t + 1 < tiles)
+            def _():
+                for copy in fetch(t + 1, 1 - slot):
+                    copy.start()
+
+            for copy in fetch(t, slot):
+                copy.wait()
+            body(t, slot)
+
+    def square_tile(t, slot):
+        @pl.loop(0, TILE_ROWS // ROWS)
+        def _(r):
+            rows = pl.ds(r * ROWS, ROWS)
+            at = pl.ds(t * TILE_ROWS + r * ROWS, ROWS)
+            gv = zbuf[slot, rows, :].astype(F32)
+            gated = ybuf[slot, rows, :].astype(F32) * (gv * jax.nn.sigmoid(gv))
+            acc[at, :] = gated
+            sqp[at, :] = lane_sum(gated * gated)
+
+    stream(square_tile)
+
+    def share(buf, send, recv):
+        buf[h] = jnp.broadcast_to(jnp.sum(sqp[...].T, axis=0, keepdims=True), (8, T))
+        for j in others:
+            remote(buf.at[h], buf.at[h], send.at[j], recv.at[h], head=h ^ j).start()
+
+    def shared(buf, send, recv):
+        for j in others:
+            remote(buf.at[h ^ j], buf.at[h ^ j], send.at[j], recv.at[h ^ j], head=h ^ j).wait_recv()
+        total = buf[0, 0:1, :]
+        for j in others:
+            total = total + buf[j, 0:1, :]
+        for j in others:
+            remote(buf.at[h], buf.at[h], send.at[j], recv.at[h], head=h ^ j).wait_send()
+        return total
+
+    share(sqx, sq_send, sq_recv)
+
     if H == 4:
         for sub in subs:
             g_arrived(1, sub, 0)
@@ -302,7 +296,17 @@
             g_to(1, sub, 1).start()
             g_to(2, sub, 0).start()
 
-
+    inv_row = lax.rsqrt(shared(sqx, sq_send, sq_recv) / DI + epsilon)
+    invc[...] = jnp.broadcast_to(inv_row, (128, T)).T
+
+    @pl.loop(0, T // ROWS)
+    def _(r):
+        at = pl.ds(r * ROWS, ROWS)
+        nbuf[at, :] = (acc[at, :] * invc[at, 0:1] * nw_ref[...]).astype(BF16)
+
+    for sub in subs:
+        for hf in range(2):
+            g_local(sub, hf).wait()
     tri = (
         lax.broadcasted_iota(jnp.int32, (CHUNK, CHUNK), 0)
         <= lax.broadcasted_iota(jnp.int32, (CHUNK, CHUNK), 1)
@@ -319,10 +323,29 @@
         == lax.broadcasted_iota(jnp.int32, (128, C), 1) // HD
     ).astype(BF16)
 
+    steps_all = [(src, dst, q) for src, dst in ((si_ref, b_ref), (so_ref, c_ref)) for q in range(chunks)]
+
+    def raw_copy(n):
+        src, _, q = steps_all[n]
+        return pltpu.make_async_copy(
+            src.at[pl.ds(q * CHUNK, CHUNK)], raw.at[n % 2], in_sem.at[0, n % 2]
+        )
+
+    raw_copy(0).start()
+    for n, (_, dst, q) in enumerate(steps_all):
+        if n + 1 < len(steps_all):
+            raw_copy(n + 1).start()
+        raw_copy(n).wait()
+        cfc[0 : CHUNK * GROUPS, :] = raw[n % 2].astype(F32).reshape(CHUNK * GROUPS, NS)
+        for g in range(NG):
+            dst[g, q * CHUNK : (q + 1) * CHUNK, :] = cfc[
+                pl.ds(first_group + g, CHUNK, stride=GROUPS), :
+            ].astype(BF16)
+
     def widen(x, g):
         high = x.astype(BF16)
         low = (x - high.astype(F32)).astype(BF16)
-        onto = spread[:, g * GW : (g + 1) * GW]
+        onto = spread[0 : x.shape[1], g * GW : (g + 1) * GW]
         return jnp.dot(high, onto, preferred_element_type=F32) + jnp.dot(
             low, onto, preferred_element_type=F32
         )
@@ -359,6 +382,19 @@
             chain.at[k, cx], chain.at[to, cx], ch_send.at[k, cx], ch_recv.at[to, cx], seq=s - 2
         )
 
+    def late_left(k, cx, n):
+        rows = pl.ds(n * (half // 2), half // 2)
+        if n:
+            send, recv = late_sem.at[0], late_sem.at[1]
+        else:
+            send, recv = ch_send.at[k, cx], ch_recv.at[Z, cx]
+        return remote(chain.at[k, cx, rows], chain.at[Z, cx, rows], send, recv, seq=s - 2)
+
+    def late_arrived(cx, n):
+        rows = pl.ds(n * (half // 2), half // 2)
+        recv = late_sem.at[1] if n else ch_recv.at[Z, cx]
+        remote(chain.at[Z, cx, rows], chain.at[Z, cx, rows], ch_send.at[0, 0], recv, seq=partner).wait_recv()
+
     def chain_arrived(k, cx):
         remote(
             chain.at[k, cx], chain.at[k, cx], ch_send.at[0, 0], ch_recv.at[k, cx], seq=partner
@@ -399,15 +435,17 @@
         return jnp.where(p <= 2 * near, close, far)
 
     def w_load(src, par, ch):
-        return pltpu.make_async_copy(src, wbuf.at[par, ch], wsem.at[par, ch])
-
-    def project(p, first):
+        return pltpu.make_async_copy(
+            src, wbuf.at[par, ch, pl.ds(0, half)], wsem.at[par, ch]
+        )
+
+    def project(p, first, parts=(0, 1)):
         k = plane_of(p)
-        for ch in range(2):
+        for ch in parts:
             w_arrived(2 * k + 1 - c, ch)
         for par in range(2):
-            for ch in range(2):
-                mine = jnp.logical_and(k == z, c == par)
+            mine = jnp.logical_and(k == z, c == par)
+            for ch in parts:
 
                 @pl.when(mine)
                 def _():
@@ -418,7 +456,7 @@
                     w_load(wfull.at[2 * k + par, ch], par, ch).start()
 
         for par in range(2):
-            for ch in range(2):
+            for ch in parts:
                 w_load(wfull.at[2 * k + par, ch], par, ch).wait()
 
         @pl.loop(0, C // TN)
@@ -426,12 +464,53 @@
             cols = pl.ds(pl.multiple_of(t * TN, TN), TN)
             total = None if first else acc[:, cols]
             for par in range(2):
-                for ch in range(2):
+                for ch in parts:
                     part = jnp.dot(
-                        gfull[2 * k + par, ch], wbuf[par, ch, :, cols], preferred_element_type=F32
+                        gfull[2 * k + par, ch],
+                        wbuf[par, ch, 0:half, cols],
+                        preferred_element_type=F32,
                     )
                     total = part if total is None else total + part
             acc[:, cols] = total
+
+    def planes_at(slot):
+        go_right = jnp.logical_and(slot > z, z < Z - 1)
+        go_left = jnp.logical_and(slot > zm, z > 0)
+        return go_right, go_left, Z + z - slot, slot - Z + z
+
+    def prep_at(i):
+        slot = i // 2
+        ch = i % 2
+        go_right, go_left, kr, kl = planes_at(slot)
+
+        @pl.when(go_right)
+        def _():
+            @pl.when(slot - 1 > z)
+            def _():
+                pair_copy(kr, 0, 0, ch).wait_send()
+
+            rs_prep(kr, half_of(kr, ch), 0, ch, 0)
+
+        @pl.when(go_left)
+        def _():
+            @pl.when(slot - 1 > zm)
+            def _():
+                pair_copy(kl, 0, 1, ch).wait_send()
+
+            rs_prep(kl, half_of(kl, ch), 1, ch, 1)
+
+    def block_of(k):
+        return 2 * k * Wr // F
+
+    cross_first = jnp.logical_or(
+        jnp.logical_and(z == 0, block_of(Z - 1) ^ h == 3),
+        jnp.logical_and(z == Z - 1, block_of(0) ^ h == 3),
+    )
+
+    def cross_arrived():
+        for sub in subs:
+            for hf in range(2):
+                g_arrived(3, sub, hf)
 
     @pl.loop(2, 2 * Z)
     def _(i):
@@ -460,14 +539,11 @@
 
             w_swap(k, ch).start()
 
-        @pl.when(i == 2)
-        def _():
-            for j in (others if H != 4 else (3,)):
-                for sub in subs:
-                    for hf in range(2):
-                        g_arrived(j, sub, hf)
-
         if H == 4:
+
+            @pl.when(jnp.logical_and(i == 2, cross_first))
+            def _():
+                cross_arrived()
 
             @pl.when(i == 3)
             def _():
@@ -475,26 +551,20 @@
                     g_arrived(1, sub, 1)
                     g_arrived(2, sub, 0)
 
-        go_right = jnp.logical_and(slot > z, z < Z - 1)
-        go_left = jnp.logical_and(slot > zm, z > 0)
-        kr = Z + z - slot
-        kl = slot - Z + z
-
-        @pl.when(go_right)
-        def _():
-            @pl.when(slot - 1 > z)
-            def _():
-                pair_copy(kr, 0, 0, ch).wait_send()
-
-            rs_prep(kr, half_of(kr, ch), 0, ch, 0)
-
-        @pl.when(go_left)
-        def _():
-            @pl.when(slot - 1 > zm)
-            def _():
-                pair_copy(kl, 0, 1, ch).wait_send()
-
-            rs_prep(kl, half_of(kl, ch), 1, ch, 1)
+        else:
+
+            @pl.when(i == 2)
+            def _():
+                for j in others:
+                    for sub in subs:
+                        for hf in range(2):
+                            g_arrived(j, sub, hf)
+
+        @pl.when(i <= 3)
+        def _():
+            prep_at(i)
+
+        go_right, go_left, kr, kl = planes_at(slot)
 
         @pl.when(go_right)
         def _():
@@ -506,23 +576,45 @@
         def _():
             cx = half_of(kl, ch)
             rs_sum(kl, cx, 1, ch, z < Z - 1)
-            chain_left(kl, cx).start()
-
-        @pl.when(i == 4)
+            late = jnp.logical_and(slot == Z - 1, ch == 1)
+
+            @pl.when(late)
+            def _():
+                late_left(kl, cx, 0).start()
+
+            @pl.when(jnp.logical_not(late))
+            def _():
+                chain_left(kl, cx).start()
+
+        if H == 4:
+
+            @pl.when(jnp.logical_and(i == 2, jnp.logical_not(cross_first)))
+            def _():
+                cross_arrived()
+
+        @pl.when(jnp.logical_and(i >= 3, i + 1 < 2 * Z))
+        def _():
+            prep_at(i + 1)
+
+        @pl.when(i == 3)
         def _():
             project(0, True)
 
         lo = jnp.where(i == 4, 1, jnp.where(i == 5, 2, slot))
-        hi = jnp.where(
-            i == 4, 2, jnp.where(i == 5, 3, jnp.where((slot >= 3) & (ch == 1), slot + 1, slot))
-        )
-        hi = jnp.where(i < 4, lo, jnp.minimum(hi, Z - 1))
+        one = jnp.logical_or(
+            jnp.logical_or(i == 4, i == 5), jnp.logical_and(slot >= 3, ch == 1)
+        )
+        hi = jnp.where(one, jnp.minimum(lo + 1, Z - 1), lo)
 
         @pl.loop(lo, hi)
         def _(p):
             project(p, False)
 
-    project(Z - 1, False)
+        @pl.when(i == 2 * Z - 2)
+        def _():
+            project(Z - 1, False, (0,))
+
+    project(Z - 1, False, (1,))
 
     @pl.loop(0, T // ROWS)
     def _(r):
@@ -530,20 +622,19 @@
         sqp[at, :] = lane_sum(acc[at, :] * nbuf[at, :].astype(F32))
 
     share(wgx, wg_send, wg_recv)
-    for ch in range(2):
-
-        @pl.when(Z - 1 > z)
-        def _():
-            pair_copy(z, ch, 0, ch).wait_send()
-
-        rs_prep(z, ch, 0, ch, ch)
-
     weighted = shared(wgx, wg_send, wg_recv) / DI
     cfc[...] = jnp.broadcast_to(weighted, (128, T)).T * invc[...] * invc[...]
 
     def put(t, slot):
         rows = pl.ds(t * TILE_ROWS, TILE_ROWS)
         return pltpu.make_async_copy(obuf.at[slot], gate_out.at[rows], out_sem.at[0, slot])
+
+    quarter = tiles // 4
+    per_quarter = T // 4 // CHUNK
+
+    def grad_at(q):
+        rows = pl.ds(pl.multiple_of((q % per_quarter) * CHUNK, CHUNK), CHUNK)
+        return q // (2 * per_quarter), (q // per_quarter) % 2, rows
 
     def grad_tile(t, slot):
         @pl.when(t >= 2)
@@ -560,7 +651,8 @@
             silu = gv * sig
             gg = invc[at, 0:1] * nw_ref[...] * acc[at, :] - values * silu * cfc[at, 0:1]
             obuf[slot, rows, :] = (gg * values * sig * (1.0 + gv * (1.0 - sig))).astype(BF16)
-            nbuf[at, :] = (gg * silu).astype(BF16)
+            here = pl.ds((t % quarter) * TILE_ROWS + r * ROWS, ROWS)
+            wbuf[t // (2 * quarter), (t // quarter) % 2, here, :] = (gg * silu).astype(BF16)
 
         put(t, slot).start()
 
@@ -589,9 +681,10 @@
         grow = jnp.exp(cum_col[at, :])
         keep = jnp.exp(jnp.broadcast_to(total, (8, 128)))
         plane, hf, rows = inside(q)
+        wa, wb, wr = grad_at(q)
         for g in range(NG):
             cols = slice(g * GW, (g + 1) * GW)
-            scaled = (widen(grow, g) * nbuf[at, cols].astype(F32)).astype(BF16)
+            scaled = (widen(grow, g) * wbuf[wa, wb, wr, cols].astype(F32)).astype(BF16)
             state = jnp.dot(c_ref[g, at, :].T, scaled, preferred_element_type=F32)
             pair[plane, hf, rows, cols] = run[:, cols].astype(BF16)
             run[:, cols] = state + widen(keep, g)[0:1, :] * run[:, cols]
@@ -667,16 +760,17 @@
 
         for part in range(PARTS):
 
-            @pl.when(q == jnp.minimum(zm + part, chunks - 1))
+            @pl.when(q == jnp.where(zm == 0, 0, jnp.minimum(2 * zm + part, chunks - 1)))
             def _():
                 state_step(part)
 
         at = pl.ds(pl.multiple_of(q * CHUNK, CHUNK), CHUNK)
         plane, hf, rows = inside(q)
+        wa, wb, wr = grad_at(q)
         cum = cum_col[at, :]
         fade = jnp.exp(last_of(q) - cum)
         steps = cfc[at, :]
-        skips = jnp.broadcast_to(skip_ref[...], (8, 128))
+        skips = jnp.broadcast_to(skip_ref[...], (8, HL))
         for g in range(NG):
             b = b_ref[g, at, :]
             scores = lax.dot_general(
@@ -693,7 +787,7 @@
                     gap = cum_row[head : head + 1, at] - cum[:, head : head + 1]
                     weights.append((scores * jnp.exp(jnp.minimum(gap, 0.0))).astype(BF16))
                 span = slice(g * GW + 2 * j * HD, g * GW + 2 * (j + 1) * HD)
-                both = nbuf[at, span]
+                both = wbuf[wa, wb, wr, span]
                 zero = jnp.zeros_like(both)
                 stacked = jnp.concatenate(
                     [jnp.where(lane < HD, both, zero), jnp.where(lane < HD, zero, both)], axis=0
@@ -701,9 +795,21 @@
                 acc[at, span] = acc[at, span] + jnp.dot(
                     jnp.concatenate(weights, axis=1), stacked, preferred_element_type=F32
                 )
-            acc[at, cols] = widen(steps, g) * acc[at, cols] + widen(skips, g)[0:1, :] * nbuf[
-                at, cols
+            acc[at, cols] = widen(steps, g) * acc[at, cols] + widen(skips, g)[0:1, :] * wbuf[
+                wa, wb, wr, cols
             ].astype(F32)
+
+    @pl.when(z > 0)
+    def _():
+        late_left(z - 1, half_of(z - 1, 1), 1).start()
+
+    for ch in range(2):
+
+        @pl.when(Z - 1 > z)
+        def _():
+            pair_copy(z, ch, 0, ch).wait_send()
+
+        rs_prep(z, ch, 0, ch, ch)
 
     @pl.when(z < Z - 1)
     def _():
@@ -778,7 +884,11 @@
             @pl.when(z != first)
             def _():
                 ch = half_of(z, step)
-                chain_arrived(from_slot, ch)
+                if first == Z - 1 and step == 1:
+                    late_arrived(ch, 0)
+                    late_arrived(ch, 1)
+                else:
+                    chain_arrived(from_slot, ch)
 
                 @pl.loop(0, half // ROWS)
                 def _(r):
@@ -832,7 +942,14 @@
             def _():
                 chain_right(k, ch).wait_send()
 
-            @pl.when(k < z)
+            late = jnp.logical_and(k == z - 1, half_of(k, 1) == ch)
+
+            @pl.when(jnp.logical_and(k < z, late))
+            def _():
+                late_left(k, ch, 0).wait_send()
+                late_left(k, ch, 1).wait_send()
+
+            @pl.when(jnp.logical_and(k < z, jnp.logical_not(late)))
             def _():
                 chain_left(k, ch).wait_send()
 
@@ -867,12 +984,6 @@
     nsub = F // Wr
     heads_here = time_step.shape[0]
     groups_here = max(1, heads_here * GROUPS // HEADS)
-    first_group = lax.axis_index("head") * heads_here // (HEADS // GROUPS)
-
-    def picked(x):
-        return lax.dynamic_slice_in_dim(x, first_group, groups_here, 1).transpose(1, 0, 2)
-
-    skip_row = jnp.pad(skip, (0, 128 - heads_here)).reshape(1, 128)
     NS = state_in.shape[2]
     hbm = pl.BlockSpec(memory_space=pl.ANY)
     vmem = pl.BlockSpec(memory_space=pltpu.VMEM)
@@ -886,7 +997,7 @@
             jax.ShapeDtypeStruct((Wr, C), F32),
             jax.ShapeDtypeStruct((S, 2, half, C), BF16),
         ),
-        in_specs=[hbm] * 4 + [vmem] * 6,
+        in_specs=[hbm] * 4 + [vmem] * 3 + [hbm] * 2 + [vmem],
         out_specs=(hbm,) * 4,
         scratch_shapes=[
             pltpu.VMEM((S, 2, T, half), BF16),
@@ -897,7 +1008,7 @@
             pltpu.VMEM((2, 2, half, C), BF16),
             pltpu.VMEM((2, half, C), F32),
             pltpu.VMEM((Wr, T), BF16),
-            pltpu.VMEM((2, 2, half, C), BF16),
+            pltpu.VMEM((2, 2, max(half, T // 4), C), BF16),
             pltpu.VMEM((2, TILE_ROWS, C), BF16),
             pltpu.VMEM((2, TILE_ROWS, C), BF16),
             pltpu.VMEM((2, TILE_ROWS, C), BF16),
@@ -915,6 +1026,9 @@
             pltpu.VMEM((2, NS, C // 2), BF16),
             pltpu.VMEM((NS, C // 2), BF16),
             pltpu.VMEM((NS, C), BF16),
+            pltpu.VMEM((2, CHUNK, GROUPS, NS), BF16),
+            pltpu.VMEM((groups_here, T, NS), BF16),
+            pltpu.VMEM((groups_here, T, NS), BF16),
             dma((S, 2)),
             dma((Z, 2)),
             dma((Z, 2)),
@@ -939,6 +1053,7 @@
             dma((4,)),
             dma((4,)),
             dma((4,)),
+            dma((2,)),
         ],
         compiler_params=pltpu.CompilerParams(
             collective_id=0, has_side_effects=True, vmem_limit_bytes=67043328
@@ -953,9 +1068,9 @@
         norm_weight.reshape(1, C),
         time_step,
         log_decay,
-        picked(state_in),
-        picked(state_out),
-        skip_row,
+        state_in,
+        state_out,
+        skip.reshape(1, heads_here),
     )
     grad_gate, grad_x, grad_out_weight, _ = outs
     return grad_x, grad_gate, grad_out_weight

time: 257 us -> 236 us (0.918)
  Pallas kernels: 239 us -> 224 us
  local copies, waits for them, and re-layouts: 16.9 us -> 10.7 us
    pallas_call x1, Pallas kernels: 239 us -> 224 us  [mixer(): pl.pallas_call(functools.partial(mixer_kernel, (S, H, T, F, Wr, C)), out_...]
    dynamic_slice x1 -> x0, local copies, waits for them, and re-layouts: 3.3 us -> none  [picked(): lax.dynamic_slice_in_dim(x, first_group, groups_here, 1).transpose(1, 0, 2)]
    unnamed x9 -> x7, local copies, waits for them, and re-layouts: 12.4 us -> 10.7 us
where the time goes in v1:
time: 236 us; the launch traced here: 235 us
  Pallas kernels  224 us (95%)
  local copies, waits for them, and re-layouts  10.7 us (5%)
    pallas_call x1, Pallas kernels, mixer(): pl.pallas_call(functools.partial(mixer_kernel, (S, H, T, F, Wr, C)), out_...  224 us
    unnamed x7, local copies, waits for them, and re-layouts  10.7 us

profile of v1, /device:TPU:0, one launch (start us, length us, event | category | flops | bytes accessed | tf_op | source)
XLA Modules:
  0.0 235.4 jit_solution(7539408450683402372)
XLA Ops:
  0.6 224.1 %mixer.1 = (bf16[1024,2048]{1,0:T(8,128)(2,1)}, bf16[1024,2048]{1,0:T(8,128)(2,1)}, f32[512,2048]{1,0:T(8,128)}, bf16[8,2,256,2048]{3,2,1,0:T(8,128)(2,1)}) custom-call(bf16[1024,1024]{1,0:T(8,128)(2,1)} %g_ref.1, bf16[512,2048]{1,0:T(8,128)(2,1)} %w_ref.1, bf16[1024,2048]{1,0:T(8,128)(2,1)} %y_ref.1, bf16[1024,2048]{1,0:T(8,128)(2,1)} %z_ref.1, ...), custom_call_target="tpu_custom_call" | custom-call | flops 34359738368 | bytes 67108864 | tf_op jit(solution)/shard_map/mixer/pallas_call | solution.py:992
  224.7 0.0 copy-start.1
  224.8 4.9 %copy.16 = bf16[1024,2048]{1,0:T(8,128)(2,1)} copy(bf16[1024,2048]{1,0:T(8,128)(2,1)} %get-tuple-element.12) | data formatting | bytes 8388608
  229.7 0.0 copy-done.1
  229.7 0.0 copy-start
  229.7 2.1 copy.17
  231.8 1.6 copy-done
  233.4 2.0 copy.18
Async XLA Ops:
  224.7 5.0 %copy-start.1 = (bf16[1024,2048]{1,0:T(8,128)(2,1)S(1)}, bf16[1024,2048]{1,0:T(8,128)(2,1)}, u32[]{:S(2)}) copy-start(bf16[1024,2048]{1,0:T(8,128)(2,1)} %get-tuple-element.13) | copy-start | bytes 12582916
  229.7 3.7 %copy-start = (f32[512,2048]{1,0:T(8,128)S(1)}, f32[512,2048]{1,0:T(8,128)}, u32[]{:S(2)}) copy-start(f32[512,2048]{1,0:T(8,128)} %get-tuple-element.14) | copy-start | bytes 12582916

commit v2 on v1

--- a/solution.py
+++ b/solution.py
@@ -760,7 +760,7 @@
 
         for part in range(PARTS):
 
-            @pl.when(q == jnp.where(zm == 0, 0, jnp.minimum(2 * zm + part, chunks - 1)))
+            @pl.when(q == jnp.where(zm == 0, 0, jnp.minimum(2 * zm + part + 1, chunks - 1)))
             def _():
                 state_step(part)
 

time: 236 us -> 238 us (level)
  no operation moved by 1% of the time
where the time goes in v2:
time: 238 us; the launch traced here: 237 us
  Pallas kernels  226 us (95%)
  local copies, waits for them, and re-layouts  10.7 us (4%)
    pallas_call x1, Pallas kernels, mixer(): pl.pallas_call(functools.partial(mixer_kernel, (S, H, T, F, Wr, C)), out_...  226 us
    unnamed x7, local copies, waits for them, and re-layouts  10.7 us

profile of v2, /device:TPU:0, one launch (start us, length us, event | category | flops | bytes accessed | tf_op | source)
XLA Modules:
  0.0 237.0 jit_solution(7270189980052757087)
XLA Ops:
  0.6 225.7 %mixer.1 = (bf16[1024,2048]{1,0:T(8,128)(2,1)}, bf16[1024,2048]{1,0:T(8,128)(2,1)}, f32[512,2048]{1,0:T(8,128)}, bf16[8,2,256,2048]{3,2,1,0:T(8,128)(2,1)}) custom-call(bf16[1024,1024]{1,0:T(8,128)(2,1)} %g_ref.1, bf16[512,2048]{1,0:T(8,128)(2,1)} %w_ref.1, bf16[1024,2048]{1,0:T(8,128)(2,1)} %y_ref.1, bf16[1024,2048]{1,0:T(8,128)(2,1)} %z_ref.1, ...), custom_call_target="tpu_custom_call" | custom-call | flops 34359738368 | bytes 67108864 | tf_op jit(solution)/shard_map/mixer/pallas_call | solution.py:992
  226.3 0.0 copy-start.1
  226.3 4.9 %copy.16 = bf16[1024,2048]{1,0:T(8,128)(2,1)} copy(bf16[1024,2048]{1,0:T(8,128)(2,1)} %get-tuple-element.12) | data formatting | bytes 8388608
  231.3 0.0 copy-done.1
  231.3 0.0 copy-start
  231.3 2.1 copy.17
  233.4 1.6 copy-done
  235.0 2.0 copy.18
Async XLA Ops:
  226.3 5.0 %copy-start.1 = (bf16[1024,2048]{1,0:T(8,128)(2,1)S(1)}, bf16[1024,2048]{1,0:T(8,128)(2,1)}, u32[]{:S(2)}) copy-start(bf16[1024,2048]{1,0:T(8,128)(2,1)} %get-tuple-element.13) | copy-start | bytes 12582916
  231.3 3.7 %copy-start = (f32[512,2048]{1,0:T(8,128)S(1)}, f32[512,2048]{1,0:T(8,128)}, u32[]{:S(2)}) copy-start(f32[512,2048]{1,0:T(8,128)} %get-tuple-element.14) | copy-start | bytes 12582916
